TPU v7x, 32 devices: a whole 2x2x4 slice. The times are simulated.
32 devices in a mesh: node: 16 (over z, y, x), hand: 2 (over core).
Axes of the slice: x: 2, y: 2, z: 4, core: 2. Of those that a mesh axis runs over, the one named last changes fastest.
Arguments:
- ranges: bfloat16 [512, 128, 1326], P('node', None, 'hand'), may hold values from 0.00019931793 to 0.0039978027
- strengths: int32 [512, 1326], P('node'), may hold values from 0 to 399
- live_hands: int32 [512, 1326], P('node'), may hold values 0 or 1
- pot_sizes: float32 [512, 128], P('node'), may hold values from 1 to 16
- action_counts: int32 [512], P('node'), may hold values from 1 to 8
- parents: int32 [512], P('node'), may hold values from 0 to 63
- turn_counts: int32 [16], replicated, may hold values from 1 to 4
- root_reach: float32 [16, 2, 1326], P(None, None, 'hand'), may hold values from 0.01 to 1
Outputs:
- turn_values: float32 [16, 2, 1326], P('node', None, 'hand')
- exploitability: float32 [], replicated
All inputs are finite; a program needn't handle non-finite values. No bound on the sum of `live_hands` on one device may be relied on, other than what follows from the above.
Results may differ from a plain program's by a relative error of at most 0.0003.
Values may be sent and summed in bfloat16 or wider, within the bound.
A program may use at most 128 MiB of HBM per device.

v0:
```python
import jax
import jax.numpy as jnp
import numpy as np
from jax import lax
from jax.sharding import PartitionSpec as P

ACT = 8
GROUPS = 8
TACT = 4


def card_pairs(wanted):
    first_list = []
    second_list = []
    for lower_card in range(52):
        for upper_card in range(lower_card + 1, 52):
            first_list.append(lower_card)
            second_list.append(upper_card)
    return (
        jnp.asarray(np.array(first_list[:wanted], dtype=np.int32)),
        jnp.asarray(np.array(second_list[:wanted], dtype=np.int32)),
    )


def pair_compat(row_first, row_second, col_first, col_second):
    shared = (row_first[:, None] == col_first[None, :]) | (
        row_first[:, None] == col_second[None, :]
    )
    shared = (
        shared
        | (row_second[:, None] == col_first[None, :])
        | (row_second[:, None] == col_second[None, :])
    )
    return jnp.where(shared, 0.0, 1.0).astype(jnp.float32)


def showdown_block(compat, packed):
    left_strength, left_live, right_strength, right_live, reach_block = packed
    signs = jnp.sign((left_strength[:, :, None] - right_strength[:, None, :]).astype(jnp.float32))
    matrix = (signs * compat[None] * left_live[:, :, None] * right_live[:, None, :]).astype(
        jnp.bfloat16
    )
    return jnp.einsum("nij,nlj->nli", matrix, reach_block, preferred_element_type=jnp.float32)


def river_from(raw_values, pots, legal):
    count = raw_values.shape[0]
    width = raw_values.shape[2]
    values = (raw_values * pots[:, :, None]).reshape(count, 2, GROUPS, ACT, width)
    usable = jnp.arange(ACT)[None, :] < legal[:, None]
    return jnp.where(usable[:, None, None, :, None], values, -1e30).max(axis=3).sum(axis=2)


def turn_best(sums, legal):
    hand_half = sums.shape[1] // 2
    shaped = sums.reshape(-1, TACT, 2, hand_half)
    usable = jnp.arange(TACT)[None, :] < legal[:, None]
    return jnp.where(usable[:, :, None, None], shaped, -1e30).max(axis=1)


def local(
    ranges, strengths, live_hands, pot_sizes, action_counts, parents, turn_counts, root_reach
):
    node_count, line_cols, hand_half = ranges.shape
    hands_all = strengths.shape[1]
    hand_start = lax.axis_index("hand") * hand_half
    first_card, second_card = card_pairs(hands_all)
    live_all = live_hands.astype(jnp.float32)
    blocks = node_count // 4

    def grouped(array):
        return array.reshape((blocks, 4) + array.shape[1:])

    row_first = lax.dynamic_slice_in_dim(first_card, hand_start, hand_half, 0)
    row_second = lax.dynamic_slice_in_dim(second_card, hand_start, hand_half, 0)
    row_strength = lax.dynamic_slice_in_dim(strengths, hand_start, hand_half, 1)
    row_live = lax.dynamic_slice_in_dim(live_all, hand_start, hand_half, 1)
    compat = pair_compat(row_first, row_second, first_card, second_card)

    def one_block(packed):
        return showdown_block(compat, packed)

    added = lax.map(
        one_block,
        (
            grouped(row_strength),
            grouped(row_live),
            grouped(strengths),
            grouped(live_all),
            grouped(lax.all_gather(ranges, "hand", axis=2, tiled=True)),
        ),
    )
    raw_values = added.reshape(jnp.zeros((node_count, line_cols, hand_half), jnp.float32).shape)
    river_best = river_from(raw_values, pot_sizes, action_counts)
    flat_best = river_best.reshape(node_count, 2 * hand_half)
    turns_all = turn_counts.shape[0]
    turns_mine = turns_all // lax.axis_size("node")
    turn_start = lax.axis_index("node") * turns_mine
    parents_all = turns_all * TACT
    onehot = (parents[None, :] == jnp.arange(parents_all, dtype=jnp.int32)[:, None]).astype(
        jnp.float32
    )
    local_sums = jnp.dot(onehot, flat_best, precision=lax.Precision.HIGHEST)
    totals = lax.psum(local_sums, "node")
    values_all = turn_best(totals, turn_counts)
    exploitability = lax.psum(jnp.sum(root_reach * values_all), "hand")
    turn_values = lax.dynamic_slice_in_dim(values_all, turn_start, turns_mine, 0)
    return (turn_values, exploitability)


def solution(mesh):
    in_specs = (
        P("node", None, "hand"),
        P("node", None),
        P("node", None),
        P("node", None),
        P("node"),
        P("node"),
        P(),
        P(None, None, "hand"),
    )
    out_specs = (P("node", None, "hand"), P())
    return jax.shard_map(local, mesh=mesh, in_specs=in_specs, out_specs=out_specs, check_vma=False)
```

profile of v0, /device:TPU:0, one launch (start us, length us, event | category | flops | bytes accessed | tf_op | source)
XLA Modules:
  0.0 278.7 jit_solution(3800787151186367840)
XLA Ops:
  7.2 0.0 all-gather.2.cloned.1.call-start
  7.2 0.7 all-gather.2.cloned.1.call-update
  7.9 0.0 all-reduce.2.cloned.1.call-start
  8.0 0.9 convert_element_type.10
  8.9 0.1 reshape.92
  9.0 0.1 constant_dynamic-slice_fusion.2
  9.1 1.0 reshape.90
  10.1 1.0 constant_dynamic-slice_fusion.3
  11.1 0.8 dynamic_slice.36
  11.9 0.8 dynamic_slice.37
  12.7 0.8 copy.23
  13.5 0.2 copy.24
  13.7 0.7 iota_compare_fusion.2
  14.4 20.9 %all-gather.2.cloned.1.call-done = bf16[32,128,1326]{1,0,2:T(8,128)(2,1)} async-done(((bf16[32,128,663]{1,0,2:T(8,128)(2,1)}), bf16[32,128,1326]{1,0,2:T(8,128)(2,1)}) %all-gather.2.cloned.1.call-update) | async-done | bytes 10862608 | tf_op jit(solution)/shard_map/all_gather | solution.py:90
  35.3 89.9 %while.11 = (s32[]{:T(128)}, f32[8,4,128,663]{2,3,1,0:T(8,128)}, bf16[8,4,128,1326]{2,1,0,3:T(4,128)(2,1)}, s32[8,4,663]{2,1,0:T(4,128)S(1)}, s32[8,4,1326]{2,1,...) while((s32[]{:T(128)}, f32[8,4,128,663]{2,3,1,0:T(8,128)}, ...), condition=%wide.region_1.2_spmd.clone, body=%wide.region_0.1_spmd.clone.sunk | while | flops 931886272 | bytes 12673953 | solution.py:83
  35.3 1.6 constant_dynamic-slice_fusion.5
  37.0 2.2 or_select_fusion.2
  39.2 7.4 %fusion.9 = f32[8,4,128,663]{2,3,1,0:T(8,128)} fusion(f32[8,4,128,663]{2,3,1,0:T(8,128)} %get-tuple-element.197, s32[]{:T(128)} %get-tuple-element.196, f32[4,1326]{1,0:T(4,128)S(1)} %dynamic-slice_bitcast_fusion.8, f32[4,663]{1,0:T(4,128)S(1)} %dynamic-slice_bitcast_fusion.9, f32[663,1326]{1,0:T(8,128)S(1)} %or_select_fusion.2, ...), kind=kOutput, calls=%fused_computation.5.clone.1 | convolution fusion | flops 924853184 | bytes 6298408 | tf_op jit(solution)/shard_map/while/body/eval_jaxpr/nij,nlj->nli/dot_general | solution.py:43
  46.6 1.6 constant_dynamic-slice_fusion.5
  48.3 2.2 or_select_fusion.2
  50.5 7.3 %fusion.9 = f32[8,4,128,663]{2,3,1,0:T(8,128)} fusion(f32[8,4,128,663]{2,3,1,0:T(8,128)} %get-tuple-element.197, s32[]{:T(128)} %get-tuple-element.196, f32[4,1326]{1,0:T(4,128)S(1)} %dynamic-slice_bitcast_fusion.8, f32[4,663]{1,0:T(4,128)S(1)} %dynamic-slice_bitcast_fusion.9, f32[663,1326]{1,0:T(8,128)S(1)} %or_select_fusion.2, ...), kind=kOutput, calls=%fused_computation.5.clone.1 | convolution fusion | flops 924853184 | bytes 6298408 | tf_op jit(solution)/shard_map/while/body/eval_jaxpr/nij,nlj->nli/dot_general | solution.py:43
  57.8 1.6 constant_dynamic-slice_fusion.5
  59.5 2.2 or_select_fusion.2
  61.7 7.3 %fusion.9 = f32[8,4,128,663]{2,3,1,0:T(8,128)} fusion(f32[8,4,128,663]{2,3,1,0:T(8,128)} %get-tuple-element.197, s32[]{:T(128)} %get-tuple-element.196, f32[4,1326]{1,0:T(4,128)S(1)} %dynamic-slice_bitcast_fusion.8, f32[4,663]{1,0:T(4,128)S(1)} %dynamic-slice_bitcast_fusion.9, f32[663,1326]{1,0:T(8,128)S(1)} %or_select_fusion.2, ...), kind=kOutput, calls=%fused_computation.5.clone.1 | convolution fusion | flops 924853184 | bytes 6298408 | tf_op jit(solution)/shard_map/while/body/eval_jaxpr/nij,nlj->nli/dot_general | solution.py:43
  69.0 1.6 constant_dynamic-slice_fusion.5
  70.7 2.2 or_select_fusion.2
  73.0 7.3 %fusion.9 = f32[8,4,128,663]{2,3,1,0:T(8,128)} fusion(f32[8,4,128,663]{2,3,1,0:T(8,128)} %get-tuple-element.197, s32[]{:T(128)} %get-tuple-element.196, f32[4,1326]{1,0:T(4,128)S(1)} %dynamic-slice_bitcast_fusion.8, f32[4,663]{1,0:T(4,128)S(1)} %dynamic-slice_bitcast_fusion.9, f32[663,1326]{1,0:T(8,128)S(1)} %or_select_fusion.2, ...), kind=kOutput, calls=%fused_computation.5.clone.1 | convolution fusion | flops 924853184 | bytes 6298408 | tf_op jit(solution)/shard_map/while/body/eval_jaxpr/nij,nlj->nli/dot_general | solution.py:43
  80.2 1.6 constant_dynamic-slice_fusion.5
  81.9 2.2 or_select_fusion.2
  84.2 7.3 %fusion.9 = f32[8,4,128,663]{2,3,1,0:T(8,128)} fusion(f32[8,4,128,663]{2,3,1,0:T(8,128)} %get-tuple-element.197, s32[]{:T(128)} %get-tuple-element.196, f32[4,1326]{1,0:T(4,128)S(1)} %dynamic-slice_bitcast_fusion.8, f32[4,663]{1,0:T(4,128)S(1)} %dynamic-slice_bitcast_fusion.9, f32[663,1326]{1,0:T(8,128)S(1)} %or_select_fusion.2, ...), kind=kOutput, calls=%fused_computation.5.clone.1 | convolution fusion | flops 924853184 | bytes 6298408 | tf_op jit(solution)/shard_map/while/body/eval_jaxpr/nij,nlj->nli/dot_general | solution.py:43
  91.5 1.6 constant_dynamic-slice_fusion.5
  93.2 2.2 or_select_fusion.2
  95.4 7.3 %fusion.9 = f32[8,4,128,663]{2,3,1,0:T(8,128)} fusion(f32[8,4,128,663]{2,3,1,0:T(8,128)} %get-tuple-element.197, s32[]{:T(128)} %get-tuple-element.196, f32[4,1326]{1,0:T(4,128)S(1)} %dynamic-slice_bitcast_fusion.8, f32[4,663]{1,0:T(4,128)S(1)} %dynamic-slice_bitcast_fusion.9, f32[663,1326]{1,0:T(8,128)S(1)} %or_select_fusion.2, ...), kind=kOutput, calls=%fused_computation.5.clone.1 | convolution fusion | flops 924853184 | bytes 6298408 | tf_op jit(solution)/shard_map/while/body/eval_jaxpr/nij,nlj->nli/dot_general | solution.py:43
  102.7 1.6 constant_dynamic-slice_fusion.5
  104.4 2.2 or_select_fusion.2
  106.7 7.3 %fusion.9 = f32[8,4,128,663]{2,3,1,0:T(8,128)} fusion(f32[8,4,128,663]{2,3,1,0:T(8,128)} %get-tuple-element.197, s32[]{:T(128)} %get-tuple-element.196, f32[4,1326]{1,0:T(4,128)S(1)} %dynamic-slice_bitcast_fusion.8, f32[4,663]{1,0:T(4,128)S(1)} %dynamic-slice_bitcast_fusion.9, f32[663,1326]{1,0:T(8,128)S(1)} %or_select_fusion.2, ...), kind=kOutput, calls=%fused_computation.5.clone.1 | convolution fusion | flops 924853184 | bytes 6298408 | tf_op jit(solution)/shard_map/while/body/eval_jaxpr/nij,nlj->nli/dot_general | solution.py:43
  113.9 1.6 constant_dynamic-slice_fusion.5
  115.6 2.2 or_select_fusion.2
  117.9 7.3 %fusion.9 = f32[8,4,128,663]{2,3,1,0:T(8,128)} fusion(f32[8,4,128,663]{2,3,1,0:T(8,128)} %get-tuple-element.197, s32[]{:T(128)} %get-tuple-element.196, f32[4,1326]{1,0:T(4,128)S(1)} %dynamic-slice_bitcast_fusion.8, f32[4,663]{1,0:T(4,128)S(1)} %dynamic-slice_bitcast_fusion.9, f32[663,1326]{1,0:T(8,128)S(1)} %or_select_fusion.2, ...), kind=kOutput, calls=%fused_computation.5.clone.1 | convolution fusion | flops 924853184 | bytes 6298408 | tf_op jit(solution)/shard_map/while/body/eval_jaxpr/nij,nlj->nli/dot_general | solution.py:43
  125.2 12.0 %copy.22 = f32[8,4,128,663]{3,2,1,0:T(8,128)} copy(f32[8,4,128,663]{2,3,1,0:T(8,128)} %get-tuple-element.44) | data formatting | bytes 21725184 | tf_op jit(solution)/shard_map/while | solution.py:83
  137.1 0.0 copy-start.1
  137.1 0.0 copy-start.2
  137.1 0.0 copy-start
  137.1 16.8 %select_reduce_fusion = f32[32,2,8,663]{3,2,1,0:T(8,128)S(1)} fusion(f32[32,2,8,8,663]{4,3,2,1,0:T(8,128)} %bitcast.31, f32[32,2,8,8]{3,2,1,0:T(8,128)S(1)} %copy.24, pred[32,8]{1,0:T(8,128)(4,1)S(1)} %iota_compare_fusion.2), kind=kLoop, calls=%fused_computation.12 | loop fusion | flops 7807488 | bytes 12237056 | tf_op jit(solution)/shard_map/reduce_max | solution.py:51
  153.9 0.5 reduce_sum.18
  154.4 0.2 reshape.94
  154.6 0.0 copy-done.1
  154.6 0.3 fusion.5
  154.9 1.1 reshape.95
  156.0 0.0 all-reduce.2.cloned.1.call-update
  156.1 0.0 copy-done.2
  156.1 0.1 iota_compare_fusion.3
  156.2 109.9 %all-reduce.2.cloned.1.call-done = f32[16,4,2,663]{3,2,1,0:T(2,128)} async-done(((f32[16,4,2,663]{3,2,1,0:T(2,128)}), f32[16,4,2,663]{3,2,1,0:T(2,128)}) %all-reduce.2.cloned.1.call-update) | async-done | bytes 339472 | tf_op jit(solution)/shard_map/psum | solution.py:104
  266.1 1.4 select_reduce_fusion.1
  267.5 0.0 copy-done
  267.5 0.7 multiply_reduce_fusion
  268.2 0.6 constant_dynamic-slice_fusion.1
  268.8 3.1 %psum.15 = f32[]{:T(128)} all-reduce(f32[]{:T(128)} %multiply_reduce_fusion), channel_id=1, replica_groups=mesh['node'=16,'hand'=2] {'hand'}, use_global_device_ids=true, to_apply=%region_7.8 | all-reduce | flops 1 | bytes 8 | tf_op jit(solution)/shard_map/psum | solution.py:106
  (35 shorter events, 0.4 us)
Async XLA Ops:
  7.2 28.1 %all-gather.2.cloned.1.call-start = ((), (), s32[]{:S(2)}) async-start(), calls=%async_computation | async-start | bytes 16293888 | tf_op jit(solution)/shard_map/all_gather | solution.py:90
  7.9 258.2 %all-reduce.2.cloned.1.call-start = ((), (), s32[]{:S(2)}) async-start(), calls=%async_computation.1 | async-start | bytes 786432 | tf_op jit(solution)/shard_map/psum | solution.py:104
  137.1 17.5 %copy-start.1 = (s32[32]{0:T(128)S(1)}, s32[32]{0:T(128)}, u32[]{:S(2)}) copy-start(s32[32]{0:T(128)} %param.17) | copy-start | bytes 388
  137.1 18.9 %copy-start.2 = (s32[16]{0:T(128)S(1)}, s32[16]{0:T(128)}, u32[]{:S(2)}) copy-start(s32[16]{0:T(128)} %param.18) | copy-start | bytes 196
  137.1 130.4 %copy-start = (f32[16,2,663]{2,1,0:T(2,128)S(1)}, f32[16,2,663]{2,1,0:T(2,128)}, u32[]{:S(2)}) copy-start(f32[16,2,663]{2,1,0:T(2,128)} %param.19) | copy-start | bytes 254596
Sparse Core Ops, SparseCore 0:
  9.5 25.7 all-gather.1
  156.2 109.8 all-reduce.1
where the time goes:
time: 280 us; the launch traced here: 279 us
  waiting for transfers between devices  132 us (47%)
  matrix products  58.7 us (21%)
  other arithmetic  39.1 us (14%)
  local copies, waits for them, and re-layouts  31.7 us (11%)
  between operations  14.2 us (5%)
  blocking collectives  3.08 us (1%)
    psum x1, waiting for transfers between devices, local(): totals = lax.psum(local_sums, 'node')  110 us
    dot_general x8, matrix products, showdown_block(): jnp.einsum('nij,nlj->nli', matrix, reach_block, preferred_element_type=jn...  58.4 us
    all_gather x1, waiting for transfers between devices, local(): lax.all_gather(ranges, 'hand', axis=2, tiled=True)  20.9 us
    select_n x8, other arithmetic, pair_compat(): return jnp.where(shared, 0.0, 1.0).astype(jnp.float32)  17.9 us
    reduce_max x1, other arithmetic, river_from(): jnp.where(usable[:, None, None, :, None], values, -1e+30).max(axis=3)  16.8 us
    dynamic_slice x8, local copies, waits for them, and re-layouts, local(): lax.map(one_block, (grouped(row_strength), grouped(row_live), grouped(str...  12.8 us
    while x1, local copies, waits for them, and re-layouts, local(): lax.map(one_block, (grouped(row_strength), grouped(row_live), grouped(str...  12 us
  transfers between devices with their start and end apart: 2, of which 2 were waited for; matrix products, arithmetic and copies ran while one was open for 2% of the time, Pallas kernels for 0%

commit v1 on v0

--- a/solution.py
+++ b/solution.py
@@ -7,6 +7,22 @@
 ACT = 8
 GROUPS = 8
 TACT = 4
+
+
+def groups_rest(mine):
+    size_here = lax.axis_size("node")
+
+    def page_bind(work_now, next_value):
+        if next_value >= size_here:
+            return work_now
+        shelf = []
+        for j in range(size_here):
+            shelf.append((j, j ^ next_value))
+        return page_bind(
+            work_now + lax.ppermute(work_now, axis_name="node", perm=shelf), 2 * next_value
+        )
+
+    return page_bind(mine, 1)
 
 
 def card_pairs(wanted):
@@ -101,7 +117,7 @@
         jnp.float32
     )
     local_sums = jnp.dot(onehot, flat_best, precision=lax.Precision.HIGHEST)
-    totals = lax.psum(local_sums, "node")
+    totals = groups_rest(local_sums)
     values_all = turn_best(totals, turn_counts)
     exploitability = lax.psum(jnp.sum(root_reach * values_all), "hand")
     turn_values = lax.dynamic_slice_in_dim(values_all, turn_start, turns_mine, 0)

time: 280 us -> 215 us (0.77)
  waiting for transfers between devices: 132 us -> 59.6 us
  starting transfers between devices: 0.08 us -> 8.19 us
    psum x1 -> x0, waiting for transfers between devices: 110 us -> none  [local(): totals = lax.psum(local_sums, 'node')]
    ppermute x0 -> x4, waiting for transfers between devices: none -> 38 us  [page_bind(): lax.ppermute(work_now, axis_name='node', perm=shelf)]
    ppermute x0 -> x4, starting transfers between devices: none -> 8.16 us  [page_bind(): lax.ppermute(work_now, axis_name='node', perm=shelf)]
  transfers between devices with their start and end apart: 2 -> 5, of which waited for: 2 -> 5; matrix products, arithmetic and copies ran while one was open for 2% -> 3% of each run, Pallas kernels for 0% -> 0%
where the time goes in v1:
time: 215 us; the launch traced here: 213 us
  waiting for transfers between devices  59.6 us (28%)
  matrix products  58.7 us (27%)
  other arithmetic  38.2 us (18%)
  local copies, waits for them, and re-layouts  31 us (14%)
  between operations  14.2 us (7%)
  starting transfers between devices  8.19 us (4%)
  blocking collectives  3.08 us (1%)
    dot_general x8, matrix products, showdown_block(): jnp.einsum('nij,nlj->nli', matrix, reach_block, preferred_element_type=jn...  58.4 us
    ppermute x4, waiting for transfers between devices, page_bind(): lax.ppermute(work_now, axis_name='node', perm=shelf)  38 us
    all_gather x1, waiting for transfers between devices, local(): lax.all_gather(ranges, 'hand', axis=2, tiled=True)  21 us
    select_n x8, other arithmetic, pair_compat(): return jnp.where(shared, 0.0, 1.0).astype(jnp.float32)  17.9 us
    reduce_max x1, other arithmetic, river_from(): jnp.where(usable[:, None, None, :, None], values, -1e+30).max(axis=3)  16.8 us
    dynamic_slice x8, local copies, waits for them, and re-layouts, local(): lax.map(one_block, (grouped(row_strength), grouped(row_live), grouped(str...  12.8 us
    while x1, local copies, waits for them, and re-layouts, local(): lax.map(one_block, (grouped(row_strength), grouped(row_live), grouped(str...  12 us
    ppermute x4, starting transfers between devices, page_bind(): lax.ppermute(work_now, axis_name='node', perm=shelf)  8.16 us
  transfers between devices with their start and end apart: 5, of which 5 were waited for; matrix products, arithmetic and copies ran while one was open for 3% of the time, Pallas kernels for 0%

profile of v1, /device:TPU:0, one launch (start us, length us, event | category | flops | bytes accessed | tf_op | source)
XLA Modules:
  0.0 213.3 jit_solution(7463860705130200226)
XLA Ops:
  7.2 0.0 all-gather.2.cloned.1.call-start
  7.2 0.7 all-gather.2.cloned.1.call-update
  7.9 0.9 convert_element_type.10
  8.9 0.1 reshape.92
  8.9 0.1 constant_dynamic-slice_fusion.2
  9.1 1.0 reshape.90
  10.0 1.0 constant_dynamic-slice_fusion.3
  11.1 0.8 dynamic_slice.36
  11.9 0.8 dynamic_slice.37
  12.6 0.8 copy.23
  13.4 0.2 copy.24
  13.6 0.7 iota_compare_fusion.2
  14.3 21.0 %all-gather.2.cloned.1.call-done = bf16[32,128,1326]{1,0,2:T(8,128)(2,1)} async-done(((bf16[32,128,663]{1,0,2:T(8,128)(2,1)}), bf16[32,128,1326]{1,0,2:T(8,128)(2,1)}) %all-gather.2.cloned.1.call-update) | async-done | bytes 10862608 | tf_op jit(solution)/shard_map/all_gather | solution.py:106
  35.3 89.9 %while.11 = (s32[]{:T(128)}, f32[8,4,128,663]{2,3,1,0:T(8,128)}, bf16[8,4,128,1326]{2,1,0,3:T(4,128)(2,1)}, s32[8,4,663]{2,1,0:T(4,128)S(1)}, s32[8,4,1326]{2,1,...) while((s32[]{:T(128)}, f32[8,4,128,663]{2,3,1,0:T(8,128)}, ...), condition=%wide.region_1.2_spmd.clone, body=%wide.region_0.1_spmd.clone.sunk | while | flops 931886272 | bytes 12673953 | solution.py:99
  35.3 1.6 constant_dynamic-slice_fusion.5
  37.0 2.2 %or_select_fusion.2 = f32[663,1326]{1,0:T(8,128)S(1)} fusion(s32[1326]{0:T(1024)} %get-tuple-element.217, s32[1326]{0:T(1024)} %get-tuple-element.216, s32[663]{0:T(1024)S(1)} %get-tuple-element.218, s32[663]{0:T(1024)S(1)} %get-tuple-element.215), kind=kLoop, calls=%fused_computation.3.clone.1 | loop fusion | flops 7033104 | bytes 3532464 | tf_op jit(solution)/shard_map/jit(_where)/select_n | solution.py:50
  39.2 7.3 %fusion.9 = f32[8,4,128,663]{2,3,1,0:T(8,128)} fusion(f32[8,4,128,663]{2,3,1,0:T(8,128)} %get-tuple-element.197, s32[]{:T(128)} %get-tuple-element.196, f32[4,1326]{1,0:T(4,128)S(1)} %dynamic-slice_bitcast_fusion.8, f32[4,663]{1,0:T(4,128)S(1)} %dynamic-slice_bitcast_fusion.9, f32[663,1326]{1,0:T(8,128)S(1)} %or_select_fusion.2, ...), kind=kOutput, calls=%fused_computation.5.clone.1 | convolution fusion | flops 924853184 | bytes 6298408 | tf_op jit(solution)/shard_map/while/body/eval_jaxpr/nij,nlj->nli/dot_general | solution.py:59
  46.6 1.6 constant_dynamic-slice_fusion.5
  48.3 2.2 %or_select_fusion.2 = f32[663,1326]{1,0:T(8,128)S(1)} fusion(s32[1326]{0:T(1024)} %get-tuple-element.217, s32[1326]{0:T(1024)} %get-tuple-element.216, s32[663]{0:T(1024)S(1)} %get-tuple-element.218, s32[663]{0:T(1024)S(1)} %get-tuple-element.215), kind=kLoop, calls=%fused_computation.3.clone.1 | loop fusion | flops 7033104 | bytes 3532464 | tf_op jit(solution)/shard_map/jit(_where)/select_n | solution.py:50
  50.5 7.3 %fusion.9 = f32[8,4,128,663]{2,3,1,0:T(8,128)} fusion(f32[8,4,128,663]{2,3,1,0:T(8,128)} %get-tuple-element.197, s32[]{:T(128)} %get-tuple-element.196, f32[4,1326]{1,0:T(4,128)S(1)} %dynamic-slice_bitcast_fusion.8, f32[4,663]{1,0:T(4,128)S(1)} %dynamic-slice_bitcast_fusion.9, f32[663,1326]{1,0:T(8,128)S(1)} %or_select_fusion.2, ...), kind=kOutput, calls=%fused_computation.5.clone.1 | convolution fusion | flops 924853184 | bytes 6298408 | tf_op jit(solution)/shard_map/while/body/eval_jaxpr/nij,nlj->nli/dot_general | solution.py:59
  57.8 1.6 constant_dynamic-slice_fusion.5
  59.5 2.2 %or_select_fusion.2 = f32[663,1326]{1,0:T(8,128)S(1)} fusion(s32[1326]{0:T(1024)} %get-tuple-element.217, s32[1326]{0:T(1024)} %get-tuple-element.216, s32[663]{0:T(1024)S(1)} %get-tuple-element.218, s32[663]{0:T(1024)S(1)} %get-tuple-element.215), kind=kLoop, calls=%fused_computation.3.clone.1 | loop fusion | flops 7033104 | bytes 3532464 | tf_op jit(solution)/shard_map/jit(_where)/select_n | solution.py:50
  61.7 7.3 %fusion.9 = f32[8,4,128,663]{2,3,1,0:T(8,128)} fusion(f32[8,4,128,663]{2,3,1,0:T(8,128)} %get-tuple-element.197, s32[]{:T(128)} %get-tuple-element.196, f32[4,1326]{1,0:T(4,128)S(1)} %dynamic-slice_bitcast_fusion.8, f32[4,663]{1,0:T(4,128)S(1)} %dynamic-slice_bitcast_fusion.9, f32[663,1326]{1,0:T(8,128)S(1)} %or_select_fusion.2, ...), kind=kOutput, calls=%fused_computation.5.clone.1 | convolution fusion | flops 924853184 | bytes 6298408 | tf_op jit(solution)/shard_map/while/body/eval_jaxpr/nij,nlj->nli/dot_general | solution.py:59
  69.0 1.6 constant_dynamic-slice_fusion.5
  70.7 2.2 %or_select_fusion.2 = f32[663,1326]{1,0:T(8,128)S(1)} fusion(s32[1326]{0:T(1024)} %get-tuple-element.217, s32[1326]{0:T(1024)} %get-tuple-element.216, s32[663]{0:T(1024)S(1)} %get-tuple-element.218, s32[663]{0:T(1024)S(1)} %get-tuple-element.215), kind=kLoop, calls=%fused_computation.3.clone.1 | loop fusion | flops 7033104 | bytes 3532464 | tf_op jit(solution)/shard_map/jit(_where)/select_n | solution.py:50
  73.0 7.3 %fusion.9 = f32[8,4,128,663]{2,3,1,0:T(8,128)} fusion(f32[8,4,128,663]{2,3,1,0:T(8,128)} %get-tuple-element.197, s32[]{:T(128)} %get-tuple-element.196, f32[4,1326]{1,0:T(4,128)S(1)} %dynamic-slice_bitcast_fusion.8, f32[4,663]{1,0:T(4,128)S(1)} %dynamic-slice_bitcast_fusion.9, f32[663,1326]{1,0:T(8,128)S(1)} %or_select_fusion.2, ...), kind=kOutput, calls=%fused_computation.5.clone.1 | convolution fusion | flops 924853184 | bytes 6298408 | tf_op jit(solution)/shard_map/while/body/eval_jaxpr/nij,nlj->nli/dot_general | solution.py:59
  80.2 1.6 constant_dynamic-slice_fusion.5
  81.9 2.2 %or_select_fusion.2 = f32[663,1326]{1,0:T(8,128)S(1)} fusion(s32[1326]{0:T(1024)} %get-tuple-element.217, s32[1326]{0:T(1024)} %get-tuple-element.216, s32[663]{0:T(1024)S(1)} %get-tuple-element.218, s32[663]{0:T(1024)S(1)} %get-tuple-element.215), kind=kLoop, calls=%fused_computation.3.clone.1 | loop fusion | flops 7033104 | bytes 3532464 | tf_op jit(solution)/shard_map/jit(_where)/select_n | solution.py:50
  84.2 7.3 %fusion.9 = f32[8,4,128,663]{2,3,1,0:T(8,128)} fusion(f32[8,4,128,663]{2,3,1,0:T(8,128)} %get-tuple-element.197, s32[]{:T(128)} %get-tuple-element.196, f32[4,1326]{1,0:T(4,128)S(1)} %dynamic-slice_bitcast_fusion.8, f32[4,663]{1,0:T(4,128)S(1)} %dynamic-slice_bitcast_fusion.9, f32[663,1326]{1,0:T(8,128)S(1)} %or_select_fusion.2, ...), kind=kOutput, calls=%fused_computation.5.clone.1 | convolution fusion | flops 924853184 | bytes 6298408 | tf_op jit(solution)/shard_map/while/body/eval_jaxpr/nij,nlj->nli/dot_general | solution.py:59
  91.5 1.6 constant_dynamic-slice_fusion.5
  93.2 2.2 %or_select_fusion.2 = f32[663,1326]{1,0:T(8,128)S(1)} fusion(s32[1326]{0:T(1024)} %get-tuple-element.217, s32[1326]{0:T(1024)} %get-tuple-element.216, s32[663]{0:T(1024)S(1)} %get-tuple-element.218, s32[663]{0:T(1024)S(1)} %get-tuple-element.215), kind=kLoop, calls=%fused_computation.3.clone.1 | loop fusion | flops 7033104 | bytes 3532464 | tf_op jit(solution)/shard_map/jit(_where)/select_n | solution.py:50
  95.4 7.3 %fusion.9 = f32[8,4,128,663]{2,3,1,0:T(8,128)} fusion(f32[8,4,128,663]{2,3,1,0:T(8,128)} %get-tuple-element.197, s32[]{:T(128)} %get-tuple-element.196, f32[4,1326]{1,0:T(4,128)S(1)} %dynamic-slice_bitcast_fusion.8, f32[4,663]{1,0:T(4,128)S(1)} %dynamic-slice_bitcast_fusion.9, f32[663,1326]{1,0:T(8,128)S(1)} %or_select_fusion.2, ...), kind=kOutput, calls=%fused_computation.5.clone.1 | convolution fusion | flops 924853184 | bytes 6298408 | tf_op jit(solution)/shard_map/while/body/eval_jaxpr/nij,nlj->nli/dot_general | solution.py:59
  102.7 1.6 constant_dynamic-slice_fusion.5
  104.4 2.2 %or_select_fusion.2 = f32[663,1326]{1,0:T(8,128)S(1)} fusion(s32[1326]{0:T(1024)} %get-tuple-element.217, s32[1326]{0:T(1024)} %get-tuple-element.216, s32[663]{0:T(1024)S(1)} %get-tuple-element.218, s32[663]{0:T(1024)S(1)} %get-tuple-element.215), kind=kLoop, calls=%fused_computation.3.clone.1 | loop fusion | flops 7033104 | bytes 3532464 | tf_op jit(solution)/shard_map/jit(_where)/select_n | solution.py:50
  106.6 7.3 %fusion.9 = f32[8,4,128,663]{2,3,1,0:T(8,128)} fusion(f32[8,4,128,663]{2,3,1,0:T(8,128)} %get-tuple-element.197, s32[]{:T(128)} %get-tuple-element.196, f32[4,1326]{1,0:T(4,128)S(1)} %dynamic-slice_bitcast_fusion.8, f32[4,663]{1,0:T(4,128)S(1)} %dynamic-slice_bitcast_fusion.9, f32[663,1326]{1,0:T(8,128)S(1)} %or_select_fusion.2, ...), kind=kOutput, calls=%fused_computation.5.clone.1 | convolution fusion | flops 924853184 | bytes 6298408 | tf_op jit(solution)/shard_map/while/body/eval_jaxpr/nij,nlj->nli/dot_general | solution.py:59
  113.9 1.6 constant_dynamic-slice_fusion.5
  115.6 2.2 %or_select_fusion.2 = f32[663,1326]{1,0:T(8,128)S(1)} fusion(s32[1326]{0:T(1024)} %get-tuple-element.217, s32[1326]{0:T(1024)} %get-tuple-element.216, s32[663]{0:T(1024)S(1)} %get-tuple-element.218, s32[663]{0:T(1024)S(1)} %get-tuple-element.215), kind=kLoop, calls=%fused_computation.3.clone.1 | loop fusion | flops 7033104 | bytes 3532464 | tf_op jit(solution)/shard_map/jit(_where)/select_n | solution.py:50
  117.8 7.3 %fusion.9 = f32[8,4,128,663]{2,3,1,0:T(8,128)} fusion(f32[8,4,128,663]{2,3,1,0:T(8,128)} %get-tuple-element.197, s32[]{:T(128)} %get-tuple-element.196, f32[4,1326]{1,0:T(4,128)S(1)} %dynamic-slice_bitcast_fusion.8, f32[4,663]{1,0:T(4,128)S(1)} %dynamic-slice_bitcast_fusion.9, f32[663,1326]{1,0:T(8,128)S(1)} %or_select_fusion.2, ...), kind=kOutput, calls=%fused_computation.5.clone.1 | convolution fusion | flops 924853184 | bytes 6298408 | tf_op jit(solution)/shard_map/while/body/eval_jaxpr/nij,nlj->nli/dot_general | solution.py:59
  125.2 12.0 %copy.22 = f32[8,4,128,663]{3,2,1,0:T(8,128)} copy(f32[8,4,128,663]{2,3,1,0:T(8,128)} %get-tuple-element.44) | data formatting | bytes 21725184 | tf_op jit(solution)/shard_map/while | solution.py:99
  137.1 0.0 copy-start.1
  137.1 0.0 copy-start.2
  137.1 0.0 copy-start
  137.1 16.8 %select_reduce_fusion = f32[32,2,8,663]{3,2,1,0:T(8,128)S(1)} fusion(f32[32,2,8,8,663]{4,3,2,1,0:T(8,128)} %bitcast.31, f32[32,2,8,8]{3,2,1,0:T(8,128)S(1)} %copy.24, pred[32,8]{1,0:T(8,128)(4,1)S(1)} %iota_compare_fusion.2), kind=kLoop, calls=%fused_computation.12 | loop fusion | flops 7807488 | bytes 12237056 | tf_op jit(solution)/shard_map/reduce_max | solution.py:67
  153.9 0.5 reduce_sum.18
  154.4 0.2 reshape.94
  154.6 0.0 copy-done.1
  154.6 0.3 fusion.5
  154.9 1.8 collective-permute-start
  156.7 8.9 %collective-permute-done = f32[64,1326]{1,0:T(8,128)S(1)} collective-permute-done((f32[64,1326]{1,0:T(8,128)S(1)}, f32[64,1326]{1,0:T(8,128)S(1)}, u32[]{:S(2)}, u32[]{:S(2)}) %collective-permute-start) | collective-permute-done | bytes 339488 | tf_op jit(solution)/shard_map/ppermute | solution.py:22
  165.6 1.8 collective-permute-start.1
  167.4 8.0 %collective-permute-done.1 = f32[64,1326]{1,0:T(8,128)S(1)} collective-permute-done((f32[64,1326]{1,0:T(8,128)S(1)}, f32[64,1326]{1,0:T(8,128)S(1)}, u32[]{:S(2)}, u32[]{:S(2)}) %collective-permute-start.1) | collective-permute-done | bytes 339488 | tf_op jit(solution)/shard_map/ppermute | solution.py:22
  175.5 1.8 collective-permute-start.2
  177.3 7.2 %collective-permute-done.2 = f32[64,1326]{1,0:T(8,128)S(1)} collective-permute-done((f32[64,1326]{1,0:T(8,128)S(1)}, f32[64,1326]{1,0:T(8,128)S(1)}, u32[]{:S(2)}, u32[]{:S(2)}) %collective-permute-start.2) | collective-permute-done | bytes 339488 | tf_op jit(solution)/shard_map/ppermute | solution.py:22
  184.5 2.7 %collective-permute-start.3 = (f32[64,1326]{1,0:T(8,128)S(1)}, f32[64,1326]{1,0:T(8,128)S(1)}, u32[]{:S(2)}, u32[]{:S(2)}) collective-permute-start(f32[64,1326]{1,0:T(8,128)S(1)} %add.29), channel_id=1, source_target_pairs={{0,16},{2,18},{4,20},{6,22},{8,24},{10,26},{12,28},{14,30},{16,0},... | collective-permute-start | bytes 1018376 | tf_op jit(solution)/shard_map/ppermute | solution.py:22
  187.2 0.0 copy-done.2
  187.2 0.1 iota_compare_fusion.3
  187.3 13.9 %collective-permute-done.3 = f32[64,1326]{1,0:T(8,128)S(1)} collective-permute-done((f32[64,1326]{1,0:T(8,128)S(1)}, f32[64,1326]{1,0:T(8,128)S(1)}, u32[]{:S(2)}, u32[]{:S(2)}) %collective-permute-start.3) | collective-permute-done | bytes 339488 | tf_op jit(solution)/shard_map/ppermute | solution.py:22
  201.3 0.4 reshape.95
  201.7 0.4 select_reduce_fusion.1
  202.1 0.0 copy-done
  202.1 0.7 multiply_reduce_fusion
  202.8 0.6 constant_dynamic-slice_fusion.1
  203.4 3.1 %psum.7 = f32[]{:T(128)} all-reduce(f32[]{:T(128)} %multiply_reduce_fusion), channel_id=1, replica_groups=mesh['node'=16,'hand'=2] {'hand'}, use_global_device_ids=true, to_apply=%region_6.7 | all-reduce | flops 1 | bytes 8 | tf_op jit(solution)/shard_map/psum | solution.py:122
  (39 shorter events, 0.6 us)
Async XLA Ops:
  7.2 28.1 %all-gather.2.cloned.1.call-start = ((), (), s32[]{:S(2)}) async-start(), calls=%async_computation | async-start | bytes 16293888 | tf_op jit(solution)/shard_map/all_gather | solution.py:106
  137.1 17.5 %copy-start.1 = (s32[32]{0:T(128)S(1)}, s32[32]{0:T(128)}, u32[]{:S(2)}) copy-start(s32[32]{0:T(128)} %param.17) | copy-start | bytes 388
  137.1 50.1 %copy-start.2 = (s32[16]{0:T(128)S(1)}, s32[16]{0:T(128)}, u32[]{:S(2)}) copy-start(s32[16]{0:T(128)} %param.18) | copy-start | bytes 196
  137.1 65.0 %copy-start = (f32[16,2,663]{2,1,0:T(2,128)S(1)}, f32[16,2,663]{2,1,0:T(2,128)}, u32[]{:S(2)}) copy-start(f32[16,2,663]{2,1,0:T(2,128)} %param.19) | copy-start | bytes 254596
  154.9 10.7 %collective-permute-start = (f32[64,1326]{1,0:T(8,128)S(1)}, f32[64,1326]{1,0:T(8,128)S(1)}, u32[]{:S(2)}, u32[]{:S(2)}) collective-permute-start(f32[64,1326]{1,0:T(8,128)S(1)} %fusion.5), channel_id=1, source_target_pairs={{0,2},{2,0},{4,6},{6,4},{8,10},{10,8},{12,14},{14,12},{16,18},{18,... | collective-permute-start | bytes 1018376 | tf_op jit(solution)/shard_map/ppermute | solution.py:22
  165.6 9.8 %collective-permute-start.1 = (f32[64,1326]{1,0:T(8,128)S(1)}, f32[64,1326]{1,0:T(8,128)S(1)}, u32[]{:S(2)}, u32[]{:S(2)}) collective-permute-start(f32[64,1326]{1,0:T(8,128)S(1)} %add.27), channel_id=1, source_target_pairs={{0,4},{2,6},{4,0},{6,2},{8,12},{10,14},{12,8},{14,10},{16,20},{18,... | collective-permute-start | bytes 1018376 | tf_op jit(solution)/shard_map/ppermute | solution.py:22
  175.5 9.0 %collective-permute-start.2 = (f32[64,1326]{1,0:T(8,128)S(1)}, f32[64,1326]{1,0:T(8,128)S(1)}, u32[]{:S(2)}, u32[]{:S(2)}) collective-permute-start(f32[64,1326]{1,0:T(8,128)S(1)} %add.28), channel_id=1, source_target_pairs={{0,8},{2,10},{4,12},{6,14},{8,0},{10,2},{12,4},{14,6},{16,24},{18,... | collective-permute-start | bytes 1018376 | tf_op jit(solution)/shard_map/ppermute | solution.py:22
  184.5 16.8 %collective-permute-start.3 = (f32[64,1326]{1,0:T(8,128)S(1)}, f32[64,1326]{1,0:T(8,128)S(1)}, u32[]{:S(2)}, u32[]{:S(2)}) collective-permute-start(f32[64,1326]{1,0:T(8,128)S(1)} %add.29), channel_id=1, source_target_pairs={{0,16},{2,18},{4,20},{6,22},{8,24},{10,26},{12,28},{14,30},{16,0},... | collective-permute-start | bytes 1018376 | tf_op jit(solution)/shard_map/ppermute | solution.py:22
Sparse Core Ops, SparseCore 0:
  9.5 25.7 all-gather.1
